TPU v7x, 32 devices: a whole 2x2x4 slice. The times are simulated.
32 devices in a mesh: dp: 4 (over x, core), band: 8 (over z, y).
Axes of the slice: x: 2, y: 2, z: 4, core: 2. Of those that a mesh axis runs over, the one named last changes fastest.
Arguments:
- features: bfloat16 [8160, 256], P(('dp', 'band')), parts along dimension 0, may hold values from -6 to 6
- corners: int32 [8160, 512], P(('dp', 'band')), parts along dimension 0, may hold values from 0 to 1535, as said below
- bilinear: float32 [8160, 512], P(('dp', 'band')), parts along dimension 0, may hold values from 0.08 to 0.5, as said below
- attention: float32 [8160, 128], P(('dp', 'band')), parts along dimension 0, may hold values from 0 to 1, as said below
- w_value: bfloat16 [256, 256], replicated, may hold values from -0.375 to 0.375
- b_value: float32 [256], replicated, may hold values from -0.6 to 0.6
- w_out: bfloat16 [256, 256], replicated, may hold values from -1.5 to 1.5
- b_out: float32 [256], replicated, may hold values from -3 to 3
- norm1_gain: float32 [256], replicated, may hold values from 0.5 to 1.5
- norm1_bias: float32 [256], replicated, may hold values from -3 to 3
- w_in: bfloat16 [256, 1024], replicated, may hold values from -0.375 to 0.375
- b_in: float32 [1024], replicated, may hold values from -3 to 3
- w_ffout: bfloat16 [1024, 256], replicated, may hold values from -0.1875 to 0.1875
- b_ffout: float32 [256], replicated, may hold values from -3 to 3
- norm2_gain: float32 [256], replicated, may hold values from 0.5 to 1.5
- norm2_bias: float32 [256], replicated, may hold values from -3 to 3
Outputs:
- encoded: bfloat16 [8160, 256], P(('dp', 'band')), parts along dimension 0
There are 4 independent parts, one for each index of `dp`. A program takes and returns all parts, laid end to end along the dimension named above; an argument that names none is the same for every part. Nothing has to cross between parts.
Inputs may be any that keep to these rules, and one draw needn't show every extreme that they name: An entry for level l is a row of a map of 192 * 8 // 4**l tokens laid out in rows of 128 // 2**l; the four corners of a point are k, k + 1, k + 128 // 2**l and k + 128 // 2**l + 1 in that order. `bilinear`: the four corner weights of a point are positive and sum to one. `attention`: for each token and head the 16 weights are positive and sum to one.
All inputs are finite; a program needn't handle non-finite values.
Results may differ from a plain program's by a relative error of at most 0.009.
Values may be sent and summed in bfloat16 or wider, within the bound.
A program may use at most 64 MiB of HBM per device.

v0:
```python
import functools

import jax
import jax.numpy as jnp
from jax import lax
from jax.experimental import pallas as pl
from jax.experimental.pallas import tpu as pltpu
from jax.sharding import PartitionSpec as P

HEADS = 8
LEVELS = 4
POINTS = 4
ROWS_DEV = 192
MAP_W = 128
LANES = 128
STRIDE = LANES - 1
CHUNK = 128
BUILT = (3, 5, 7, 8)

F32 = jnp.float32
BF16 = jnp.bfloat16
MESH = pl.DeviceIdType.MESH


def plan(bands):
    rows = [ROWS_DEV // 4**level for level in range(LEVELS)]
    starts = [sum(rows[:level]) for level in range(LEVELS)]
    widths = [MAP_W // 2**level for level in range(LEVELS)]
    lengths = [count * bands for count in rows]
    merged, used = {}, 0
    for level in reversed(range(LEVELS)):
        if used + lengths[level] <= LANES:
            merged[level] = used
            used += lengths[level]
        else:
            break
    windowed = [level for level in range(LEVELS) if level not in merged]
    groups = {level: (lengths[level] - widths[level] - 2) // STRIDE + 1 for level in windowed}
    return rows, starts, widths, lengths, merged, windowed, groups


def flat_lanes(length, width, groups):
    need = STRIDE * (groups - 1) + width + LANES
    return -(-max(length, need) // LANES) * LANES


def norm(inputs, gain, shift):
    average = jnp.mean(inputs, axis=-1, keepdims=True)
    centred = inputs - average
    variance = jnp.mean(centred * centred, axis=-1, keepdims=True)
    return centred * lax.rsqrt(variance + 1e-05) * gain + shift


def one_hot_pair(iota, place, weights):
    low = iota == place
    high = iota == place + 1.0
    zero = jnp.zeros((), F32)
    top = jnp.where(low, weights[0], jnp.where(high, weights[1], zero))
    bottom = jnp.where(low, weights[2], jnp.where(high, weights[3], zero))
    return top, bottom


def kernel(
    bands,
    feat,
    corners_hbm,
    bilinear_hbm,
    attention_hbm,
    w_value_hbm,
    b_value,
    w_out_hbm,
    b_out,
    gain1,
    bias1,
    w_in_hbm,
    b_in,
    w_ff_hbm,
    b_ff,
    gain2,
    bias2,
    out,
    gathered,
    values,
    corners,
    bilinear,
    attention,
    w_value,
    w_value_t,
    shift_t,
    place_t,
    group_t,
    bil_t,
    att_t,
    hot,
    hot_merged,
    table_merged,
    samp_t,
    w_out,
    w_in,
    w_ff,
    send_sem,
    recv_sem,
    load_sem,
    *level_scratch,
):
    rows, starts, widths, lengths, merged, windowed, groups = plan(bands)
    flats = level_scratch[:LEVELS]
    tables = dict(zip(windowed, level_scratch[LEVELS:]))
    tokens, model = feat.shape
    head_dim = model // HEADS
    padded = place_t.shape[1]
    me = lax.axis_index("band")

    line = bands // 2
    mine_z, mine_y = me // 2, lax.rem(me, 2)
    partner = mine_z * 2 + 1 - mine_y
    has_left, has_right = mine_z > 0, mine_z < line - 1
    cuts = [(begin, min(begin + CHUNK, tokens) - begin) for begin in range(0, tokens, CHUNK)]

    sources = (corners_hbm, bilinear_hbm, attention_hbm, w_value_hbm, w_out_hbm, w_in_hbm, w_ff_hbm)
    targets = (corners, bilinear, attention, w_value, w_out, w_in, w_ff)
    loads = [
        pltpu.make_async_copy(source, target, load_sem.at[number])
        for number, (source, target) in enumerate(zip(sources, targets))
    ]

    barrier = pltpu.get_barrier_semaphore()

    def greet(target):
        pl.semaphore_signal(barrier, inc=1, device_id={"band": target}, device_id_type=MESH)

    greet(partner)
    pl.when(has_left)(lambda: greet(me - 2))
    pl.when(has_right)(lambda: greet(me + 2))
    pl.semaphore_wait(
        barrier, 1 + has_left.astype(jnp.int32) + has_right.astype(jnp.int32)
    )

    def copy_of(source, block, cut, target, lane):
        begin, count = cuts[cut]
        return pltpu.make_async_remote_copy(
            src_ref=source.at[pl.ds(begin, count)],
            dst_ref=gathered.at[block, pl.ds(begin, count)],
            send_sem=send_sem.at[lane, block, cut],
            recv_sem=recv_sem.at[block, cut],
            device_id={"band": target},
            device_id_type=MESH,
        )

    def moves(block, cut, source=None):
        source = gathered.at[block] if source is None else source
        left = copy_of(source, block, cut, me - 2, 0)
        right = copy_of(source, block, cut, me + 2, 1)
        across = copy_of(source, block, cut, partner, 2)
        return left, right, across

    for cut in range(len(cuts)):
        left, right, across = moves(me, cut, feat)
        pl.when(has_left)(left.start)
        pl.when(has_right)(right.start)
        across.start()
    for load in loads:
        load.start()

    def project(rows_in, block):
        value_t = lax.dot_general(
            w_value_t[...], rows_in, (((1,), (1,)), ((), ())), preferred_element_type=F32
        )
        values[block, :, 0:tokens] = (value_t + shift_t[:, 0:1]).astype(BF16).astype(F32)

    def stage(distance, cut):
        before, after = me - 2 * distance, me + 2 * distance

        @pl.when(mine_z >= distance)
        def _():
            left, right, across = moves(before, cut)
            across.wait_recv()
            pl.when(has_right)(right.start)
            across.start()

        @pl.when(mine_z + distance < line)
        def _():
            left, right, across = moves(after, cut)
            across.wait_recv()
            pl.when(has_left)(left.start)
            across.start()

        if cut == len(cuts) - 1:
            pl.when(mine_z >= distance)(lambda: project(gathered[before], before))
            pl.when(mine_z + distance < line)(lambda: project(gathered[after], after))

    def arrive(block):
        for cut in range(len(cuts)):
            moves(block, cut)[2].wait_recv()
        project(gathered[block], block)

    def finish(block, came_left, came_right, own=False):
        for cut in range(len(cuts)):
            left, right, across = moves(block, cut, feat if own else None)
            if own or came_right:
                pl.when(has_left)(left.wait_send)
            if own or came_left:
                pl.when(has_right)(right.wait_send)
            across.wait_send()

    for load in loads[:4]:
        load.wait()
    w_value_t[...] = jnp.transpose(w_value[...].astype(F32)).astype(BF16)
    shift_t[...] = jnp.transpose(jnp.broadcast_to(b_value[...], (LANES, model)))

    def turned(block):
        tail = jnp.zeros((padded - tokens, block.shape[1]), F32)
        return jnp.transpose(jnp.concatenate([block, tail], axis=0))

    corner_t = turned(corners[...].astype(F32))
    group_t[...] = jnp.floor((corner_t + 0.5) * (1.0 / STRIDE))
    place_t[...] = corner_t
    bil_t[...] = turned(bilinear[...])
    att_t[...] = turned(attention[...])
    for level in range(LEVELS):
        flats[level][...] = jnp.zeros(flats[level].shape, F32)

    iota = lax.broadcasted_iota(jnp.int32, (LANES, padded), 0).astype(F32)

    def point_weights(point):
        share = att_t[pl.ds(point, 1), :]
        return [
            (share * bil_t[pl.ds(point * 4 + corner, 1), :]).astype(BF16).astype(F32)
            for corner in range(4)
        ]

    def build(head, carry):
        for slot, level in enumerate(windowed):
            for which in range(POINTS):
                point = (head * LEVELS + level) * POINTS + which
                place = place_t[pl.ds(point * 4, 1), :] - STRIDE * group_t[pl.ds(point * 4, 1), :]
                top, bottom = one_hot_pair(iota, place, point_weights(point))
                hot[head, slot * POINTS + which, 0:LANES, :] = top.astype(BF16)
                hot[head, slot * POINTS + which, LANES:, :] = bottom.astype(BF16)
        top_sum = jnp.zeros((LANES, padded), F32)
        bottom_sum = jnp.zeros((LANES, padded), F32)
        for level in merged:
            for which in range(POINTS):
                point = (head * LEVELS + level) * POINTS + which
                place = place_t[pl.ds(point * 4, 1), :] + float(merged[level])
                top, bottom = one_hot_pair(iota, place, point_weights(point))
                top_sum += top
                bottom_sum += bottom
        hot_merged[head, 0:LANES, :] = top_sum.astype(BF16)
        hot_merged[head, LANES:, :] = bottom_sum.astype(BF16)
        return carry

    stages = [(distance, cut) for distance in range(1, line) for cut in range(len(cuts))]
    done = 0
    for number, entry in enumerate(stages):
        upto = min(HEADS, BUILT[min(number, len(BUILT) - 1)])
        if upto > done:
            lax.fori_loop(done, upto, build, 0)
            done = upto
        if number == 0:
            project(feat[...], me)
        stage(*entry)
    if done < HEADS:
        lax.fori_loop(done, HEADS, build, 0)
    arrive(partner)
    for distance in range(1, line):
        pl.when(mine_z >= distance)(functools.partial(arrive, partner - 2 * distance))
        pl.when(mine_z + distance < line)(functools.partial(arrive, partner + 2 * distance))

    for band in range(bands):
        value_t = values[band]
        for level in range(LEVELS):
            count = rows[level]
            flats[level][:, band * count : (band + 1) * count] = value_t[
                :, starts[level] : starts[level] + count
            ]

    for level in windowed:
        for group in range(groups[level]):
            base = STRIDE * group
            top = flats[level][:, base : base + LANES].astype(BF16)
            under = base + widths[level]
            bottom = flats[level][:, under : under + LANES].astype(BF16)
            for head in range(HEADS):
                part = slice(head * head_dim, (head + 1) * head_dim)
                into = slice(group * head_dim, (group + 1) * head_dim)
                tables[level][head, into, 0:LANES] = top[part, :]
                tables[level][head, into, LANES:] = bottom[part, :]
    lane = lax.broadcasted_iota(jnp.int32, (1, LANES), 1)
    top = jnp.zeros((model, LANES), F32)
    bottom = jnp.zeros((model, LANES), F32)
    for level, begin in merged.items():
        inside = (lane >= begin) & (lane < begin + lengths[level])
        piece = flats[level][:, 0:LANES]
        top += jnp.where(inside, pltpu.roll(piece, begin, 1), 0.0)
        bottom += jnp.where(
            inside, pltpu.roll(piece, (begin - widths[level]) % LANES, 1), 0.0
        )
    for head in range(HEADS):
        part = slice(head * head_dim, (head + 1) * head_dim)
        table_merged[head, :, 0:LANES] = top[part, :].astype(BF16)
        table_merged[head, :, LANES:] = bottom[part, :].astype(BF16)

    def blend(head, carry):
        total = jnp.dot(table_merged[head], hot_merged[head], preferred_element_type=F32)
        for slot, level in enumerate(windowed):
            for which in range(POINTS):
                point = (head * LEVELS + level) * POINTS + which
                mine = group_t[pl.ds(point * 4, 1), :]
                picked = jnp.dot(
                    tables[level][head],
                    hot[head, slot * POINTS + which],
                    preferred_element_type=F32,
                )
                for group in range(groups[level]):
                    total += jnp.where(
                        mine == float(group),
                        picked[group * head_dim : (group + 1) * head_dim, :],
                        0.0,
                    )
        samp_t[pl.ds(pl.multiple_of(head * head_dim, head_dim), head_dim), :] = total
        return carry

    lax.fori_loop(0, HEADS, blend, 0)

    for load in loads[4:]:
        load.wait()
    sampled = jnp.transpose(samp_t[...])[0:tokens, :].astype(BF16)
    attended = jnp.dot(sampled, w_out[...], preferred_element_type=F32) + b_out[...]
    middle = norm(feat[...].astype(F32) + attended, gain1[...], bias1[...]).astype(BF16)
    hidden = jnp.maximum(
        jnp.dot(middle, w_in[...], preferred_element_type=F32) + b_in[...], 0.0
    ).astype(BF16)
    result = (
        middle.astype(F32)
        + jnp.dot(hidden, w_ff[...], preferred_element_type=F32)
        + b_ff[...]
    )
    out[...] = norm(result, gain2[...], bias2[...]).astype(BF16)
    finish(me, False, False, own=True)
    for distance in range(1, line):
        pl.when(mine_z >= distance)(
            functools.partial(finish, me - 2 * distance, True, False)
        )
        pl.when(mine_z + distance < line)(
            functools.partial(finish, me + 2 * distance, False, True)
        )


def body(bands, *args):
    feat, corners = args[0], args[1]
    tokens, model = feat.shape
    padded = -(-tokens // LANES) * LANES
    rows, starts, widths, lengths, merged, windowed, groups = plan(bands)
    head_dim = model // HEADS
    samples = corners.shape[1]
    operands = [
        argument.reshape(1, -1) if argument.ndim == 1 else argument for argument in args
    ]
    anywhere = {1, 2, 3, 4, 6, 10, 12}
    cuts = -(-tokens // CHUNK)
    specs = [
        pl.BlockSpec(memory_space=pl.ANY if number in anywhere else pltpu.VMEM)
        for number in range(len(operands))
    ]
    flat_shapes = [
        pltpu.VMEM(
            (model, flat_lanes(lengths[level], widths[level], groups.get(level, 1))), F32
        )
        for level in range(LEVELS)
    ]
    table_shapes = [
        pltpu.VMEM((HEADS, groups[level] * head_dim, 2 * LANES), BF16) for level in windowed
    ]
    scratch = [
        pltpu.VMEM((bands, tokens, model), BF16),
        pltpu.VMEM((bands, model, padded), F32),
        pltpu.VMEM(args[1].shape, jnp.int32),
        pltpu.VMEM(args[2].shape, F32),
        pltpu.VMEM(args[3].shape, F32),
        pltpu.VMEM(args[4].shape, BF16),
        pltpu.VMEM(args[4].shape, BF16),
        pltpu.VMEM((model, LANES), F32),
        pltpu.VMEM((samples, padded), F32),
        pltpu.VMEM((samples, padded), F32),
        pltpu.VMEM((samples, padded), F32),
        pltpu.VMEM((samples // 4, padded), F32),
        pltpu.VMEM((HEADS, len(windowed) * POINTS, 2 * LANES, padded), BF16),
        pltpu.VMEM((HEADS, 2 * LANES, padded), BF16),
        pltpu.VMEM((HEADS, head_dim, 2 * LANES), BF16),
        pltpu.VMEM((model, padded), F32),
        pltpu.VMEM(args[6].shape, BF16),
        pltpu.VMEM(args[10].shape, BF16),
        pltpu.VMEM(args[12].shape, BF16),
        pltpu.SemaphoreType.DMA((3, bands, cuts)),
        pltpu.SemaphoreType.DMA((bands, cuts)),
        pltpu.SemaphoreType.DMA((len(anywhere),)),
    ] + flat_shapes + table_shapes
    return pl.pallas_call(
        functools.partial(kernel, bands),
        out_shape=jax.ShapeDtypeStruct((tokens, model), BF16),
        in_specs=specs,
        out_specs=pl.BlockSpec(memory_space=pltpu.VMEM),
        scratch_shapes=scratch,
        compiler_params=pltpu.CompilerParams(
            collective_id=0, has_side_effects=True, vmem_limit_bytes=60 * 1024 * 1024
        ),
        name="layer",
    )(*operands)


def solution(mesh):
    split = P(("dp", "band"), None)
    in_specs = (split,) * 4 + (P(),) * 12
    return jax.shard_map(
        functools.partial(body, mesh.shape["band"]),
        mesh=mesh,
        in_specs=in_specs,
        out_specs=split,
        check_vma=False,
    )
```

profile of v0, /device:TPU:0, one launch (start us, length us, event | category | flops | bytes accessed | tf_op | source)
XLA Modules:
  0.0 31.2 jit_solution(14436328508894404972)
XLA Ops:
  0.0 29.7 %layer.1 = bf16[255,256]{1,0:T(8,128)(2,1)} custom-call(bf16[255,256]{1,0:T(8,128)(2,1)} %feat.1, s32[255,512]{1,0:T(8,128)} %corners_hbm.1, f32[255,512]{1,0:T(8,128)} %bilinear_hbm.1, f32[255,128]{1,0:T(8,128)} %attention_hbm.1, bf16[256,256]{1,0:T(8,128)(2,1)} %w_value_hbm.1, f32[1,256]{1,0:T(1,128)} %bitcast.9, bf16[256,256]{1,0:T(8,128)(2,1)} %w_out_hbm.1, ...), custom_call_target="tpu_custom_call" | custom-call | tf_op jit(solution)/shard_map/layer/pallas_call | solution.py:399
  29.7 1.6 %copy.18 = bf16[255,256]{1,0:T(8,128)(2,1)} copy(bf16[255,256]{1,0:T(8,128)(2,1)} %layer.1) | data formatting | bytes 261120
where the time goes:
time: 31.4 us; the launch traced here: 31.2 us
  Pallas kernels  29.7 us (95%)
  local copies, waits for them, and re-layouts  1.57 us (5%)
    pallas_call x1, Pallas kernels, body(): pl.pallas_call(functools.partial(kernel, bands), out_shape=jax.ShapeDtype...  29.7 us
    unnamed x1, local copies, waits for them, and re-layouts  1.57 us

commit v1 on v0

v1 whole, which is shorter than its diff:
```python
import functools

import jax
import jax.numpy as jnp
from jax import lax
from jax.experimental import pallas as pl
from jax.experimental.pallas import tpu as pltpu
from jax.sharding import PartitionSpec as P

HEADS = 8
LEVELS = 4
POINTS = 4
ROWS_DEV = 192
MAP_W = 128
LANES = 128
UNIT = 16
CHUNK = 128
BUILT = (5, 9, 12, 14)

F32 = jnp.float32
BF16 = jnp.bfloat16
MESH = pl.DeviceIdType.MESH


def norm(inputs, gain, shift):
    average = jnp.mean(inputs, axis=-1, keepdims=True)
    centred = inputs - average
    variance = jnp.mean(centred * centred, axis=-1, keepdims=True)
    return centred * lax.rsqrt(variance + 1e-05) * gain + shift


def kernel(
    bands,
    feat_hbm,
    corners_hbm,
    bilinear_hbm,
    attention_hbm,
    w_value_hbm,
    b_value_hbm,
    w_out_hbm,
    b_out_hbm,
    gain1_hbm,
    bias1_hbm,
    w_in_hbm,
    b_in_hbm,
    w_ff_hbm,
    b_ff_hbm,
    gain2_hbm,
    bias2_hbm,
    out,
    gathered,
    corners,
    bilinear,
    attention,
    w_value,
    b_value,
    w_out,
    b_out,
    gain1,
    bias1,
    w_in,
    b_in,
    w_ff,
    b_ff,
    gain2,
    bias2,
    w_value_t,
    shift_t,
    turned_t,
    row_t,
    column_t,
    row_next_t,
    column_next_t,
    place_t,
    weight_t,
    matrix,
    samp_t,
    send_sem,
    recv_sem,
    load_sem,
):
    rows = [ROWS_DEV // 4**level for level in range(LEVELS)]
    starts = [sum(rows[:level]) for level in range(LEVELS)]
    widths = [MAP_W // 2**level for level in range(LEVELS)]
    tokens, model = feat_hbm.shape
    head_dim = model // HEADS
    padded = matrix.shape[3]
    halves = matrix.shape[2]
    points = HEADS * LEVELS * POINTS
    me = lax.axis_index("band")

    line = bands // 2
    mine_z, mine_y = me // 2, lax.rem(me, 2)
    partner = mine_z * 2 + 1 - mine_y
    has_left, has_right = mine_z > 0, mine_z < line - 1
    cuts = [(begin, min(begin + CHUNK, tokens) - begin) for begin in range(0, tokens, CHUNK)]

    barrier = pltpu.get_barrier_semaphore()

    def greet(target):
        pl.semaphore_signal(barrier, inc=1, device_id={"band": target}, device_id_type=MESH)

    greet(partner)
    pl.when(has_left)(lambda: greet(me - 2))
    pl.when(has_right)(lambda: greet(me + 2))

    sources = (
        feat_hbm, corners_hbm, bilinear_hbm, attention_hbm, w_value_hbm, b_value_hbm,
        w_out_hbm, b_out_hbm, gain1_hbm, bias1_hbm, w_in_hbm, b_in_hbm, w_ff_hbm, b_ff_hbm,
        gain2_hbm, bias2_hbm,
    )
    targets = (
        gathered.at[me], corners, bilinear, attention, w_value, b_value,
        w_out, b_out, gain1, bias1, w_in, b_in, w_ff, b_ff, gain2, bias2,
    )
    loads = [
        pltpu.make_async_copy(source, target, load_sem.at[number])
        for number, (source, target) in enumerate(zip(sources, targets))
    ]
    for load in loads:
        load.start()

    def copy_of(block, cut, target, lane):
        begin, count = cuts[cut]
        part = gathered.at[block, pl.ds(begin, count)]
        return pltpu.make_async_remote_copy(
            src_ref=part,
            dst_ref=part,
            send_sem=send_sem.at[lane, block, cut],
            recv_sem=recv_sem.at[block, cut],
            device_id={"band": target},
            device_id_type=MESH,
        )

    both = jnp.minimum(mine_z, line - 1 - mine_z)
    more_right = mine_z * 2 < line

    def arrival(number):
        paired = number <= 2 * both
        from_left = jnp.where(paired, number % 2 == 1, jnp.logical_not(more_right))
        distance = jnp.where(paired, (number + 1) // 2, number - both)
        return from_left, mine_z + jnp.where(from_left, -distance, distance)

    def onward(number):
        from_left, place = arrival(number)
        target = jnp.where(from_left, me + 2, me - 2)
        exists = jnp.where(from_left, has_right, has_left)
        return place * 2 + mine_y, place * 2 + 1 - mine_y, target, exists

    loads[0].wait()
    pl.semaphore_wait(
        barrier, 1 + has_left.astype(jnp.int32) + has_right.astype(jnp.int32)
    )
    for cut in range(len(cuts)):
        pl.when(has_left)(copy_of(me, cut, me - 2, 0).start)
        pl.when(has_right)(copy_of(me, cut, me + 2, 1).start)
        copy_of(me, cut, partner, 2).start()

    def forward(number, cut):
        block, _, target, exists = onward(number)
        copy_of(block, cut, partner, 2).wait_recv()
        pl.when(exists)(copy_of(block, cut, target, 0).start)
        copy_of(block, cut, partner, 2).start()

    for load in loads[1:6]:
        load.wait()
    w_value_t[...] = jnp.transpose(w_value[...].astype(F32)).astype(BF16)
    shift_t[...] = jnp.transpose(jnp.broadcast_to(b_value[...], (LANES, model)))

    def turned(block):
        tail = jnp.zeros((padded - tokens, block.shape[1]), F32)
        table = jnp.transpose(jnp.concatenate([block, tail], axis=0))
        return [table[:, half * LANES : (half + 1) * LANES] for half in range(halves)]

    for half, table in enumerate(turned(corners[...].astype(F32))):
        turned_t[half] = table
    level_of = lax.broadcasted_iota(jnp.int32, (points, LANES), 0) // POINTS % LEVELS
    width_of = jnp.where(level_of == 0, float(widths[0]), float(widths[1]))
    inverse = jnp.where(level_of == 0, 1.0 / widths[0], 1.0 / widths[1])
    for half in range(halves):
        place = turned_t[half, pl.ds(0, points, stride=4), :]
        place_t[half] = place
        row = jnp.floor((place + 0.5) * inverse)
        row_t[half] = row
        column_t[half] = place - row * width_of
        row = jnp.floor((place + 1.5) * inverse)
        row_next_t[half] = row
        column_next_t[half] = place + 1.0 - row * width_of
    for half, table in enumerate(turned(bilinear[...])):
        turned_t[half] = table
    for half, share in enumerate(turned(attention[...])):
        for corner in range(4):
            product = share * turned_t[half, pl.ds(corner, points, stride=4), :]
            weight_t[corner, half] = product.astype(BF16).astype(F32)
    samp_t[...] = jnp.zeros(samp_t.shape, F32)

    iota = lax.broadcasted_iota(jnp.int32, (UNIT, LANES), 0).astype(F32)
    zero = jnp.zeros((UNIT, LANES), BF16)

    def spread(table, *at):
        *lead, point = at
        return jnp.broadcast_to(table[(*lead, pl.ds(point, 1), slice(None))], (UNIT, LANES))

    def build(piece, carry):
        head, half = piece // halves, piece % halves
        for level in (0, 1):
            width, count = widths[level], rows[level]
            total = count * bands // width
            base = (head * LEVELS + level) * POINTS
            spans = min(width, 4 * UNIT)
            own_row = [spread(row_t, half, base + which).astype(BF16) for which in range(POINTS)]
            own_column = [
                spread(column_t, half, base + which).astype(BF16) for which in range(POINTS)
            ]
            next_row = [
                spread(row_next_t, half, base + which).astype(BF16) for which in range(POINTS)
            ]
            next_column = [
                spread(column_next_t, half, base + which).astype(BF16) for which in range(POINTS)
            ]
            weight = [
                [spread(weight_t, corner, half, base + which).astype(BF16) for corner in range(4)]
                for which in range(POINTS)
            ]
            for first in range(0, width, spans):
                top, bottom = [], []
                for unit in range(first, first + spans, UNIT):
                    at = (iota + float(unit)).astype(BF16)
                    for which in range(POINTS):
                        left = at == own_column[which]
                        right = at == next_column[which]
                        w = weight[which]
                        top.append(jnp.where(left, w[0], jnp.where(right, w[1], zero)))
                        bottom.append(jnp.where(left, w[2], jnp.where(right, w[3], zero)))
                before = None
                for row in range(total):
                    now = [value == float(row) for value in own_row]
                    turn = [value == float(row) for value in next_row] if first == 0 else now
                    for number in range(spans // UNIT):
                        masks = turn if number == 0 else now
                        earlier = None if before is None else before[0 if number == 0 else 1]
                        entry = None
                        for which in range(POINTS):
                            index = number * POINTS + which
                            under = (
                                zero
                                if earlier is None
                                else jnp.where(earlier[which], bottom[index], zero)
                            )
                            term = jnp.where(masks[which], top[index], under)
                            entry = term if entry is None else entry + term
                        place = row * width + first + number * UNIT
                        block, inside = place // count, starts[level] + place % count
                        matrix[block, head, half, inside : inside + UNIT, :] = entry
                    before = (turn, now)
        exact = max(rows[2], rows[3]) * bands <= 256
        kind = BF16 if exact else F32
        begin = padded - UNIT
        row_at = iota + float(begin)
        third = row_at < float(starts[3])
        valid = row_at < float(starts[3] + rows[3])
        unit_zero = jnp.zeros((UNIT, LANES), kind)

        def mixed(table, *at):
            pair = [
                spread(table, *at, (head * LEVELS + level) * POINTS + which) for level in (2, 3)
            ]
            return jnp.where(third, pair[0], pair[1]).astype(kind)

        coarse = []
        for which in range(POINTS):
            coarse.append(
                (
                    mixed(place_t, half),
                    [mixed(weight_t, corner, half) for corner in range(4)],
                )
            )
        for block in range(bands):
            position = jnp.where(
                third,
                row_at + float(block * rows[2] - starts[2]),
                jnp.where(valid, row_at + float(block * rows[3] - starts[3]), -1000.0),
            )
            under = position - jnp.where(third, float(widths[2]), float(widths[3]))
            spots = [
                spot.astype(kind) for spot in (position, position - 1.0, under, under - 1.0)
            ]
            entry = None
            for place, weights in coarse:
                term = unit_zero
                for spot, weight in zip(spots, weights):
                    term = jnp.where(spot == place, weight, term)
                entry = term if entry is None else entry + term
            matrix[block, head, half, begin:padded, :] = entry.astype(BF16)
        return carry

    lane = lax.broadcasted_iota(jnp.int32, (model, LANES), 1)

    def consume(block):
        value_t = lax.dot_general(
            w_value_t[...], gathered[block], (((1,), (1,)), ((), ())), preferred_element_type=F32
        )
        pieces = []
        for half in range(halves):
            stop = min(tokens, (half + 1) * LANES)
            part = value_t[:, half * LANES : stop]
            count = stop - half * LANES
            if count < LANES:
                part = jnp.concatenate(
                    [part, jnp.zeros((model, LANES - count), F32)], axis=1
                )
            part = part + shift_t[...]
            if count < LANES:
                part = jnp.where(lane < count, part, 0.0)
            pieces.append(part.astype(BF16))
        value = jnp.concatenate(pieces, axis=1)
        for head in range(HEADS):
            into = slice(head * head_dim, (head + 1) * head_dim)
            lookup = jnp.concatenate([matrix[block, head, half] for half in range(halves)], axis=1)
            samp_t[into, :] += jnp.dot(value[into, :], lookup, preferred_element_type=F32)

    stages = [(number, cut) for number in range(1, line) for cut in range(len(cuts))]
    everything = HEADS * halves
    done = 0
    ready = []
    for index, (number, cut) in enumerate(stages):
        upto = everything if index >= len(BUILT) else min(everything, BUILT[index])
        if upto > done:
            lax.fori_loop(done, upto, build, 0)
            done = upto
            if done == everything:
                consume(me)
        elif ready:
            consume(ready.pop(0))
        forward(number, cut)
        if cut == len(cuts) - 1:
            ready.append(onward(number)[0])
    if done < everything:
        lax.fori_loop(done, everything, build, 0)
        consume(me)
    across = [partner] + [onward(number)[1] for number in range(1, line)]

    def consume_across(block):
        for cut in range(len(cuts)):
            copy_of(block, cut, partner, 2).wait_recv()
        consume(block)

    for block in across[:-1]:
        consume_across(block)
        if ready:
            consume(ready.pop(0))
    for block in ready:
        consume(block)
    consume_across(across[-1])

    for load in loads[6:]:
        load.wait()
    sampled = jnp.transpose(samp_t[...])[0:tokens, :].astype(BF16)
    attended = jnp.dot(sampled, w_out[...], preferred_element_type=F32) + b_out[...]
    middle = norm(gathered[me].astype(F32) + attended, gain1[...], bias1[...]).astype(BF16)
    hidden = jnp.maximum(
        jnp.dot(middle, w_in[...], preferred_element_type=F32) + b_in[...], 0.0
    ).astype(BF16)
    result = (
        middle.astype(F32)
        + jnp.dot(hidden, w_ff[...], preferred_element_type=F32)
        + b_ff[...]
    )
    out[...] = norm(result, gain2[...], bias2[...]).astype(BF16)

    for cut in range(len(cuts)):
        pl.when(has_left)(copy_of(me, cut, me - 2, 0).wait_send)
        pl.when(has_right)(copy_of(me, cut, me + 2, 1).wait_send)
        copy_of(me, cut, partner, 2).wait_send()
        for number in range(1, line):
            block, _, target, exists = onward(number)
            pl.when(exists)(copy_of(block, cut, target, 0).wait_send)
            copy_of(block, cut, partner, 2).wait_send()


def body(bands, *args):
    tokens, model = args[0].shape
    padded = -(-tokens // LANES) * LANES
    halves = padded // LANES
    samples = args[1].shape[1]
    points = samples // 4
    operands = [
        argument.reshape(1, -1) if argument.ndim == 1 else argument for argument in args
    ]
    cuts = -(-tokens // CHUNK)
    table = pltpu.VMEM((halves, points, LANES), F32)
    scratch = [
        pltpu.VMEM((bands, tokens, model), BF16),
        *(pltpu.VMEM(operand.shape, operand.dtype) for operand in operands[1:]),
        pltpu.VMEM(args[4].shape, BF16),
        pltpu.VMEM((model, LANES), F32),
        pltpu.VMEM((halves, samples, LANES), F32),
        table,
        table,
        table,
        table,
        table,
        pltpu.VMEM((4, halves, points, LANES), F32),
        pltpu.VMEM((bands, HEADS, halves, padded, LANES), BF16),
        pltpu.VMEM((model, padded), F32),
        pltpu.SemaphoreType.DMA((3, bands, cuts)),
        pltpu.SemaphoreType.DMA((bands, cuts)),
        pltpu.SemaphoreType.DMA((len(operands),)),
    ]
    return pl.pallas_call(
        functools.partial(kernel, bands),
        out_shape=jax.ShapeDtypeStruct((tokens, model), BF16),
        in_specs=[pl.BlockSpec(memory_space=pl.ANY)] * len(operands),
        out_specs=pl.BlockSpec(memory_space=pltpu.VMEM),
        scratch_shapes=scratch,
        compiler_params=pltpu.CompilerParams(
            collective_id=0, has_side_effects=True, vmem_limit_bytes=60 * 1024 * 1024
        ),
        name="layer",
    )(*operands)


def solution(mesh):
    split = P(("dp", "band"), None)
    in_specs = (split,) * 4 + (P(),) * 12
    return jax.shard_map(
        functools.partial(body, mesh.shape["band"]),
        mesh=mesh,
        in_specs=in_specs,
        out_specs=split,
        check_vma=False,
    )
```

time: 31.4 us -> 25.8 us (0.82)
  Pallas kernels: 29.7 us -> 24 us
    pallas_call x1, Pallas kernels: 29.7 us -> 24 us  [body(): pl.pallas_call(functools.partial(kernel, bands), out_shape=jax.ShapeDtype...]
where the time goes in v1:
time: 25.8 us; the launch traced here: 25.6 us
  Pallas kernels  24 us (93%)
  local copies, waits for them, and re-layouts  1.57 us (6%)
    pallas_call x1, Pallas kernels, body(): pl.pallas_call(functools.partial(kernel, bands), out_shape=jax.ShapeDtype...  24 us
    unnamed x1, local copies, waits for them, and re-layouts  1.57 us

profile of v1, /device:TPU:0, one launch (start us, length us, event | category | flops | bytes accessed | tf_op | source)
XLA Modules:
  0.0 25.6 jit_solution(5712426028644871690)
XLA Ops:
  0.0 24.0 %layer.1 = bf16[255,256]{1,0:T(8,128)(2,1)} custom-call(bf16[255,256]{1,0:T(8,128)(2,1)} %feat_hbm.1, s32[255,512]{1,0:T(8,128)} %corners_hbm.1, f32[255,512]{1,0:T(8,128)} %bilinear_hbm.1, f32[255,128]{1,0:T(8,128)} %attention_hbm.1, bf16[256,256]{1,0:T(8,128)(2,1)} %w_value_hbm.1, f32[1,256]{1,0:T(1,128)} %bitcast.9, bf16[256,256]{1,0:T(8,128)(2,1)} %w_out_hbm.1, ...), custom_call_target="tpu_custom_call" | custom-call | tf_op jit(solution)/shard_map/layer/pallas_call | solution.py:410
  24.0 1.6 %copy.18 = bf16[255,256]{1,0:T(8,128)(2,1)} copy(bf16[255,256]{1,0:T(8,128)(2,1)} %layer.1) | data formatting | bytes 261120

commit v2 on v1

--- a/solution.py
+++ b/solution.py
@@ -14,8 +14,8 @@
 MAP_W = 128
 LANES = 128
 UNIT = 16
-CHUNK = 128
-BUILT = (5, 9, 12, 14)
+CHUNK = 64
+AHEAD = 6
 
 F32 = jnp.float32
 BF16 = jnp.bfloat16
@@ -75,8 +75,10 @@
     weight_t,
     matrix,
     samp_t,
-    send_sem,
+    line_sem,
+    across_sem,
     recv_sem,
+    cross_sem,
     load_sem,
 ):
     rows = [ROWS_DEV // 4**level for level in range(LEVELS)]
@@ -92,7 +94,6 @@
     line = bands // 2
     mine_z, mine_y = me // 2, lax.rem(me, 2)
     partner = mine_z * 2 + 1 - mine_y
-    has_left, has_right = mine_z > 0, mine_z < line - 1
     cuts = [(begin, min(begin + CHUNK, tokens) - begin) for begin in range(0, tokens, CHUNK)]
 
     barrier = pltpu.get_barrier_semaphore()
@@ -100,9 +101,15 @@
     def greet(target):
         pl.semaphore_signal(barrier, inc=1, device_id={"band": target}, device_id_type=MESH)
 
+    at_start, at_stop = mine_z == 0, mine_z == line - 1
+    direct = [(mine_z > 0, me - 2), (mine_z < line - 1, me + 2)]
+    greeted = [*direct]
+    if line > 2:
+        direct.append((at_stop, mine_y))
+        greeted.append((at_start, (line - 1) * 2 + mine_y))
     greet(partner)
-    pl.when(has_left)(lambda: greet(me - 2))
-    pl.when(has_right)(lambda: greet(me + 2))
+    for exists, target in greeted:
+        pl.when(exists)(functools.partial(greet, target))
 
     sources = (
         feat_hbm, corners_hbm, bilinear_hbm, attention_hbm, w_value_hbm, b_value_hbm,
@@ -120,47 +127,60 @@
     for load in loads:
         load.start()
 
-    def copy_of(block, cut, target, lane):
-        begin, count = cuts[cut]
-        part = gathered.at[block, pl.ds(begin, count)]
+    def move(part, target, send, receive):
         return pltpu.make_async_remote_copy(
             src_ref=part,
             dst_ref=part,
-            send_sem=send_sem.at[lane, block, cut],
-            recv_sem=recv_sem.at[block, cut],
+            send_sem=send,
+            recv_sem=receive,
             device_id={"band": target},
             device_id_type=MESH,
         )
 
+    def along_line(block, cut, target, way):
+        part = gathered.at[block, pl.ds(*cuts[cut])] if cut is not None else gathered.at[block]
+        receive = recv_sem.at[block // 2, cut or 0]
+        return move(part, target, line_sem.at[way], receive)
+
+    def across(block, cut, way):
+        part = gathered.at[block, pl.ds(*cuts[cut])] if cut is not None else gathered.at[block]
+        return move(part, partner, across_sem.at[way], cross_sem.at[block // 2])
+
     both = jnp.minimum(mine_z, line - 1 - mine_z)
     more_right = mine_z * 2 < line
 
     def arrival(number):
         paired = number <= 2 * both
-        from_left = jnp.where(paired, number % 2 == 1, jnp.logical_not(more_right))
+        from_left = jnp.where(paired, number % 2 == 0, jnp.logical_not(more_right))
         distance = jnp.where(paired, (number + 1) // 2, number - both)
-        return from_left, mine_z + jnp.where(from_left, -distance, distance)
-
-    def onward(number):
-        from_left, place = arrival(number)
-        target = jnp.where(from_left, me + 2, me - 2)
-        exists = jnp.where(from_left, has_right, has_left)
-        return place * 2 + mine_y, place * 2 + 1 - mine_y, target, exists
+        skipped = line - 1 if number == 2 else max(number - 1, 1)
+        distance = jnp.where(at_start, skipped, distance)
+        place = mine_z + jnp.where(from_left, -distance, distance)
+        onto = jnp.where(from_left, mine_z + 1, mine_z - 1)
+        exists = jnp.logical_and(onto >= 0, onto < line)
+        if line > 2:
+            exists = jnp.logical_and(exists, onto - place != 1 - line)
+        return place, exists, onto * 2 + mine_y
+
+    arrivals = [arrival(number) for number in range(1, line)]
+    near = [place * 2 + mine_y for place, _, _ in arrivals]
+    far = [place * 2 + 1 - mine_y for place, _, _ in arrivals]
 
     loads[0].wait()
-    pl.semaphore_wait(
-        barrier, 1 + has_left.astype(jnp.int32) + has_right.astype(jnp.int32)
-    )
+    pl.semaphore_wait(barrier, 1 + sum(exists.astype(jnp.int32) for exists, _ in direct))
     for cut in range(len(cuts)):
-        pl.when(has_left)(copy_of(me, cut, me - 2, 0).start)
-        pl.when(has_right)(copy_of(me, cut, me + 2, 1).start)
-        copy_of(me, cut, partner, 2).start()
+        for way in reversed(range(len(direct))):
+            exists, target = direct[way]
+            pl.when(exists)(along_line(me, cut, target, way).start)
+        across(me, cut, 0).start()
 
     def forward(number, cut):
-        block, _, target, exists = onward(number)
-        copy_of(block, cut, partner, 2).wait_recv()
-        pl.when(exists)(copy_of(block, cut, target, 0).start)
-        copy_of(block, cut, partner, 2).start()
+        block = near[number]
+        _, exists, target = arrivals[number]
+        copy = along_line(block, cut, target, len(direct) + number)
+        copy.wait_recv()
+        pl.when(exists)(copy.start)
+        across(block, cut, 1 + number).start()
 
     for load in loads[1:6]:
         load.wait()
@@ -319,39 +339,30 @@
             lookup = jnp.concatenate([matrix[block, head, half] for half in range(halves)], axis=1)
             samp_t[into, :] += jnp.dot(value[into, :], lookup, preferred_element_type=F32)
 
-    stages = [(number, cut) for number in range(1, line) for cut in range(len(cuts))]
+    def consume_across(block):
+        across(block, None, 0).wait_recv()
+        consume(block)
+
     everything = HEADS * halves
     done = 0
-    ready = []
-    for index, (number, cut) in enumerate(stages):
-        upto = everything if index >= len(BUILT) else min(everything, BUILT[index])
+    for index, (cut, number) in enumerate(
+        [(cut, number) for cut in range(len(cuts)) for number in range(min(2, line - 1))]
+        + [(cut, number) for number in range(2, line - 1) for cut in range(len(cuts))]
+    ):
+        upto = min(everything, AHEAD + index)
         if upto > done:
             lax.fori_loop(done, upto, build, 0)
             done = upto
-            if done == everything:
-                consume(me)
-        elif ready:
-            consume(ready.pop(0))
         forward(number, cut)
-        if cut == len(cuts) - 1:
-            ready.append(onward(number)[0])
     if done < everything:
         lax.fori_loop(done, everything, build, 0)
-        consume(me)
-    across = [partner] + [onward(number)[1] for number in range(1, line)]
-
-    def consume_across(block):
-        for cut in range(len(cuts)):
-            copy_of(block, cut, partner, 2).wait_recv()
-        consume(block)
-
-    for block in across[:-1]:
-        consume_across(block)
-        if ready:
-            consume(ready.pop(0))
-    for block in ready:
-        consume(block)
-    consume_across(across[-1])
+    consume(me)
+    consume_across(partner)
+    for number in range(line - 1):
+        consume(near[number])
+        if number:
+            consume_across(far[number - 1])
+    consume_across(far[line - 2])
 
     for load in loads[6:]:
         load.wait()
@@ -368,14 +379,14 @@
     )
     out[...] = norm(result, gain2[...], bias2[...]).astype(BF16)
 
-    for cut in range(len(cuts)):
-        pl.when(has_left)(copy_of(me, cut, me - 2, 0).wait_send)
-        pl.when(has_right)(copy_of(me, cut, me + 2, 1).wait_send)
-        copy_of(me, cut, partner, 2).wait_send()
-        for number in range(1, line):
-            block, _, target, exists = onward(number)
-            pl.when(exists)(copy_of(block, cut, target, 0).wait_send)
-            copy_of(block, cut, partner, 2).wait_send()
+    for way, (exists, target) in enumerate(direct):
+        pl.when(exists)(along_line(me, None, target, way).wait_send)
+    across(me, None, 0).wait_send()
+    for number, (_, exists, target) in enumerate(arrivals):
+        pl.when(exists)(
+            along_line(near[number], None, target, len(direct) + number).wait_send
+        )
+        across(near[number], None, 1 + number).wait_send()
 
 
 def body(bands, *args):
@@ -403,10 +414,14 @@
         pltpu.VMEM((4, halves, points, LANES), F32),
         pltpu.VMEM((bands, HEADS, halves, padded, LANES), BF16),
         pltpu.VMEM((model, padded), F32),
-        pltpu.SemaphoreType.DMA((3, bands, cuts)),
-        pltpu.SemaphoreType.DMA((bands, cuts)),
+        pltpu.SemaphoreType.DMA((2 + bands // 2,)),
+        pltpu.SemaphoreType.DMA((bands // 2,)),
+        pltpu.SemaphoreType.DMA((bands // 2, cuts)),
+        pltpu.SemaphoreType.DMA((bands // 2,)),
         pltpu.SemaphoreType.DMA((len(operands),)),
     ]
+    held = bands * HEADS * padded * padded * 2 + bands * tokens * model * 2
+    limit = held + 16 * 1024 * 1024
     return pl.pallas_call(
         functools.partial(kernel, bands),
         out_shape=jax.ShapeDtypeStruct((tokens, model), BF16),
@@ -414,10 +429,10 @@
         out_specs=pl.BlockSpec(memory_space=pltpu.VMEM),
         scratch_shapes=scratch,
         compiler_params=pltpu.CompilerParams(
-            collective_id=0, has_side_effects=True, vmem_limit_bytes=60 * 1024 * 1024
+            collective_id=0, has_side_effects=True, vmem_limit_bytes=limit
         ),
         name="layer",
-    )(*operands)
+    )(*(pltpu.with_memory_space_constraint(operand, pltpu.HBM) for operand in operands))
 
 
 def solution(mesh):

time: 25.8 us -> 21.2 us (0.82)
  Pallas kernels: 24 us -> 20.3 us
  local copies, waits for them, and re-layouts: 1.57 us -> 0.66 us
    pallas_call x1, Pallas kernels: 24 us -> 20.3 us  [body(): pl.pallas_call(functools.partial(kernel, bands), out_shape=jax.ShapeDtype...]
    unnamed x1, local copies, waits for them, and re-layouts: 1.57 us -> 0.66 us
where the time goes in v2:
time: 21.2 us; the launch traced here: 21 us
  Pallas kernels  20.3 us (96%)
  local copies, waits for them, and re-layouts  0.66 us (3%)
    pallas_call x1, Pallas kernels, body(): pl.pallas_call(functools.partial(kernel, bands), out_shape=jax.ShapeDtype...  20.3 us
    unnamed x1, local copies, waits for them, and re-layouts  0.66 us

profile of v2, /device:TPU:0, one launch (start us, length us, event | category | flops | bytes accessed | tf_op | source)
XLA Modules:
  0.0 21.0 jit_solution(1080388865279378773)
XLA Ops:
  0.0 20.3 %layer.1 = bf16[255,256]{1,0:T(8,128)(2,1)S(1)} custom-call(bf16[255,256]{1,0:T(8,128)(2,1)} %feat_hbm.1, s32[255,512]{1,0:T(8,128)} %corners_hbm.1, f32[255,512]{1,0:T(8,128)} %bilinear_hbm.1, f32[255,128]{1,0:T(8,128)} %attention_hbm.1, bf16[256,256]{1,0:T(8,128)(2,1)} %w_value_hbm.1, f32[1,256]{1,0:T(1,128)} %bitcast.9, bf16[256,256]{1,0:T(8,128)(2,1)} %w_out_hbm.1, ...), custom_call_target="tpu_custom_call" | custom-call | tf_op jit(solution)/shard_map/layer/pallas_call | solution.py:425
  20.3 0.7 %copy.18 = bf16[255,256]{1,0:T(8,128)(2,1)} copy(bf16[255,256]{1,0:T(8,128)(2,1)S(1)} %layer.1) | data formatting | bytes 261120

commit v3 on v2

--- a/solution.py
+++ b/solution.py
@@ -15,6 +15,7 @@
 LANES = 128
 UNIT = 16
 CHUNK = 64
+SLANTED = 3
 AHEAD = 6
 
 F32 = jnp.float32
@@ -107,7 +108,10 @@
     if line > 2:
         direct.append((at_stop, mine_y))
         greeted.append((at_start, (line - 1) * 2 + mine_y))
+    slanted = [(at_stop, 1 - mine_y)] if line > 2 else []
     greet(partner)
+    if line > 2:
+        greeted.append((at_start, line * 2 - 1 - mine_y))
     for exists, target in greeted:
         pl.when(exists)(functools.partial(greet, target))
 
@@ -146,6 +150,13 @@
         part = gathered.at[block, pl.ds(*cuts[cut])] if cut is not None else gathered.at[block]
         return move(part, partner, across_sem.at[way], cross_sem.at[block // 2])
 
+    later = pl.ds(cuts[SLANTED][0], tokens - cuts[SLANTED][0])
+    sooner = pl.ds(0, cuts[SLANTED][0])
+
+    def slant(cut, target):
+        part = gathered.at[me, pl.ds(*cuts[cut]) if cut is not None else later]
+        return move(part, target, line_sem.at[2 * line], cross_sem.at[mine_z])
+
     both = jnp.minimum(mine_z, line - 1 - mine_z)
     more_right = mine_z * 2 < line
 
@@ -167,12 +178,19 @@
     far = [place * 2 + 1 - mine_y for place, _, _ in arrivals]
 
     loads[0].wait()
-    pl.semaphore_wait(barrier, 1 + sum(exists.astype(jnp.int32) for exists, _ in direct))
+    pl.semaphore_wait(barrier, 1 + sum(exists.astype(jnp.int32) for exists, _ in [*direct, *slanted]))
     for cut in range(len(cuts)):
-        for way in reversed(range(len(direct))):
+        for way in range(2):
             exists, target = direct[way]
             pl.when(exists)(along_line(me, cut, target, way).start)
         across(me, cut, 0).start()
+    for cut in range(len(cuts)):
+        for way in range(2, len(direct)):
+            exists, target = direct[way]
+            pl.when(exists)(along_line(me, cut, target, way).start)
+        if cut >= SLANTED:
+            for exists, target in slanted:
+                pl.when(exists)(slant(cut, target).start)
 
     def forward(number, cut):
         block = near[number]
@@ -180,7 +198,11 @@
         copy = along_line(block, cut, target, len(direct) + number)
         copy.wait_recv()
         pl.when(exists)(copy.start)
-        across(block, cut, 1 + number).start()
+        if line > 2 and cut >= SLANTED:
+            spared = jnp.logical_and(at_start, block // 2 == line - 1)
+            pl.when(jnp.logical_not(spared))(across(block, cut, 1 + number).start)
+        else:
+            across(block, cut, 1 + number).start()
 
     for load in loads[1:6]:
         load.wait()
@@ -346,8 +368,7 @@
     everything = HEADS * halves
     done = 0
     for index, (cut, number) in enumerate(
-        [(cut, number) for cut in range(len(cuts)) for number in range(min(2, line - 1))]
-        + [(cut, number) for number in range(2, line - 1) for cut in range(len(cuts))]
+        (cut, number) for number in range(line - 1) for cut in range(len(cuts))
     ):
         upto = min(everything, AHEAD + index)
         if upto > done:
@@ -366,8 +387,9 @@
 
     for load in loads[6:]:
         load.wait()
-    sampled = jnp.transpose(samp_t[...])[0:tokens, :].astype(BF16)
-    attended = jnp.dot(sampled, w_out[...], preferred_element_type=F32) + b_out[...]
+    attended = lax.dot_general(
+        samp_t[...].astype(BF16), w_out[...], (((0,), (0,)), ((), ())), preferred_element_type=F32
+    )[0:tokens, :] + b_out[...]
     middle = norm(gathered[me].astype(F32) + attended, gain1[...], bias1[...]).astype(BF16)
     hidden = jnp.maximum(
         jnp.dot(middle, w_in[...], preferred_element_type=F32) + b_in[...], 0.0
@@ -386,7 +408,18 @@
         pl.when(exists)(
             along_line(near[number], None, target, len(direct) + number).wait_send
         )
-        across(near[number], None, 1 + number).wait_send()
+        block = near[number]
+        if line > 2:
+            spared = jnp.logical_and(at_start, block // 2 == line - 1)
+            part = gathered.at[block, sooner]
+            pl.when(jnp.logical_not(spared))(across(block, None, 1 + number).wait_send)
+            pl.when(spared)(
+                move(part, partner, across_sem.at[1 + number], cross_sem.at[0]).wait_send
+            )
+        else:
+            across(block, None, 1 + number).wait_send()
+    for exists, target in slanted:
+        pl.when(exists)(slant(None, target).wait_send)
 
 
 def body(bands, *args):
@@ -414,7 +447,7 @@
         pltpu.VMEM((4, halves, points, LANES), F32),
         pltpu.VMEM((bands, HEADS, halves, padded, LANES), BF16),
         pltpu.VMEM((model, padded), F32),
-        pltpu.SemaphoreType.DMA((2 + bands // 2,)),
+        pltpu.SemaphoreType.DMA((bands + 1,)),
         pltpu.SemaphoreType.DMA((bands // 2,)),
         pltpu.SemaphoreType.DMA((bands // 2, cuts)),
         pltpu.SemaphoreType.DMA((bands // 2,)),

time: 21.2 us -> 20.9 us (0.986)
    pallas_call x1, Pallas kernels: 20.3 us -> 20.1 us  [body(): pl.pallas_call(functools.partial(kernel, bands), out_shape=jax.ShapeDtype...]
where the time goes in v3:
time: 20.9 us; the launch traced here: 20.7 us
  Pallas kernels  20.1 us (96%)
  local copies, waits for them, and re-layouts  0.66 us (3%)
    pallas_call x1, Pallas kernels, body(): pl.pallas_call(functools.partial(kernel, bands), out_shape=jax.ShapeDtype...  20.1 us
    unnamed x1, local copies, waits for them, and re-layouts  0.66 us

profile of v3, /device:TPU:0, one launch (start us, length us, event | category | flops | bytes accessed | tf_op | source)
XLA Modules:
  0.0 20.7 jit_solution(12720800628562928594)
XLA Ops:
  0.0 20.1 %layer.1 = bf16[255,256]{1,0:T(8,128)(2,1)S(1)} custom-call(bf16[255,256]{1,0:T(8,128)(2,1)} %feat_hbm.1, s32[255,512]{1,0:T(8,128)} %corners_hbm.1, f32[255,512]{1,0:T(8,128)} %bilinear_hbm.1, f32[255,128]{1,0:T(8,128)} %attention_hbm.1, bf16[256,256]{1,0:T(8,128)(2,1)} %w_value_hbm.1, f32[1,256]{1,0:T(1,128)} %bitcast.9, bf16[256,256]{1,0:T(8,128)(2,1)} %w_out_hbm.1, ...), custom_call_target="tpu_custom_call" | custom-call | tf_op jit(solution)/shard_map/layer/pallas_call | solution.py:458
  20.1 0.7 %copy.18 = bf16[255,256]{1,0:T(8,128)(2,1)} copy(bf16[255,256]{1,0:T(8,128)(2,1)S(1)} %layer.1) | data formatting | bytes 261120

commit v4 on v2

--- a/solution.py
+++ b/solution.py
@@ -15,6 +15,7 @@
 LANES = 128
 UNIT = 16
 CHUNK = 64
+LATE = 2
 AHEAD = 6
 
 F32 = jnp.float32
@@ -80,6 +81,7 @@
     recv_sem,
     cross_sem,
     load_sem,
+    late_sem,
 ):
     rows = [ROWS_DEV // 4**level for level in range(LEVELS)]
     starts = [sum(rows[:level]) for level in range(LEVELS)]
@@ -169,10 +171,33 @@
     loads[0].wait()
     pl.semaphore_wait(barrier, 1 + sum(exists.astype(jnp.int32) for exists, _ in direct))
     for cut in range(len(cuts)):
-        for way in reversed(range(len(direct))):
+        for way in range(2):
             exists, target = direct[way]
             pl.when(exists)(along_line(me, cut, target, way).start)
         across(me, cut, 0).start()
+    for cut in range(len(cuts)):
+        for way in range(2, len(direct)):
+            exists, target = direct[way]
+            pl.when(exists)(along_line(me, cut, target, way).start)
+
+    later = pl.ds(cuts[LATE][0], tokens - cuts[LATE][0])
+    sooner = pl.ds(0, cuts[LATE][0])
+    second = jnp.logical_and(mine_z == 1, line > 2)
+    bridge = jnp.logical_and(second, mine_y == 0)
+
+    def across_late(block, part):
+        return move(gathered.at[block, part], partner, late_sem.at[0], late_sem.at[1])
+
+    def across_soon(block, way):
+        part = gathered.at[block, sooner]
+        return move(part, partner, across_sem.at[way], cross_sem.at[block // 2])
+
+    def bridged(block):
+        part = gathered.at[block, later]
+        return move(part, me - 2, late_sem.at[2], cross_sem.at[block // 2])
+
+    def spared(number):
+        return jnp.logical_and(me == 1, near[number] // 2 == 2)
 
     def forward(number, cut):
         block = near[number]
@@ -180,7 +205,13 @@
         copy = along_line(block, cut, target, len(direct) + number)
         copy.wait_recv()
         pl.when(exists)(copy.start)
-        across(block, cut, 1 + number).start()
+        if cut < LATE:
+            across(block, cut, 1 + number).start()
+        elif number == 0:
+            pl.when(second)(across_late(block, pl.ds(*cuts[cut])).start)
+            pl.when(jnp.logical_not(second))(across(block, cut, 1 + number).start)
+        else:
+            pl.when(jnp.logical_not(spared(number)))(across(block, cut, 1 + number).start)
 
     for load in loads[1:6]:
         load.wait()
@@ -343,16 +374,29 @@
         across(block, None, 0).wait_recv()
         consume(block)
 
+    def consume_first_across():
+        block = far[0]
+        pl.when(jnp.logical_not(second))(across(block, None, 0).wait_recv)
+        pl.when(second)(across_soon(block, 0).wait_recv)
+        pl.when(jnp.logical_and(second, mine_y == 1))(across_late(block, later).wait_recv)
+        consume(block)
+
     everything = HEADS * halves
     done = 0
     for index, (cut, number) in enumerate(
-        [(cut, number) for cut in range(len(cuts)) for number in range(min(2, line - 1))]
-        + [(cut, number) for number in range(2, line - 1) for cut in range(len(cuts))]
+        (cut, number) for number in range(line - 1) for cut in range(len(cuts))
     ):
         upto = min(everything, AHEAD + index)
         if upto > done:
             lax.fori_loop(done, upto, build, 0)
             done = upto
+        if number == 2 and cut == 0:
+
+            @pl.when(bridge)
+            def _():
+                across_late(far[0], later).wait_recv()
+                bridged(far[0]).start()
+
         forward(number, cut)
     if done < everything:
         lax.fori_loop(done, everything, build, 0)
@@ -360,14 +404,17 @@
     consume_across(partner)
     for number in range(line - 1):
         consume(near[number])
-        if number:
+        if number == 1:
+            consume_first_across()
+        elif number:
             consume_across(far[number - 1])
     consume_across(far[line - 2])
 
     for load in loads[6:]:
         load.wait()
-    sampled = jnp.transpose(samp_t[...])[0:tokens, :].astype(BF16)
-    attended = jnp.dot(sampled, w_out[...], preferred_element_type=F32) + b_out[...]
+    attended = lax.dot_general(
+        samp_t[...].astype(BF16), w_out[...], (((0,), (0,)), ((), ())), preferred_element_type=F32
+    )[0:tokens, :] + b_out[...]
     middle = norm(gathered[me].astype(F32) + attended, gain1[...], bias1[...]).astype(BF16)
     hidden = jnp.maximum(
         jnp.dot(middle, w_in[...], preferred_element_type=F32) + b_in[...], 0.0
@@ -386,7 +433,11 @@
         pl.when(exists)(
             along_line(near[number], None, target, len(direct) + number).wait_send
         )
-        across(near[number], None, 1 + number).wait_send()
+        short = second if number == 0 else spared(number)
+        pl.when(short)(across_soon(near[number], 1 + number).wait_send)
+        pl.when(jnp.logical_not(short))(across(near[number], None, 1 + number).wait_send)
+    pl.when(second)(across_late(near[0], later).wait_send)
+    pl.when(bridge)(bridged(far[0]).wait_send)
 
 
 def body(bands, *args):
@@ -419,6 +470,7 @@
         pltpu.SemaphoreType.DMA((bands // 2, cuts)),
         pltpu.SemaphoreType.DMA((bands // 2,)),
         pltpu.SemaphoreType.DMA((len(operands),)),
+        pltpu.SemaphoreType.DMA((3,)),
     ]
     held = bands * HEADS * padded * padded * 2 + bands * tokens * model * 2
     limit = held + 16 * 1024 * 1024

time: 21.2 us -> 19.9 us (0.939)
  Pallas kernels: 20.3 us -> 19.1 us
    pallas_call x1, Pallas kernels: 20.3 us -> 19.1 us  [body(): pl.pallas_call(functools.partial(kernel, bands), out_shape=jax.ShapeDtype...]
where the time goes in v4:
time: 19.9 us; the launch traced here: 19.8 us
  Pallas kernels  19.1 us (96%)
  local copies, waits for them, and re-layouts  0.66 us (3%)
    pallas_call x1, Pallas kernels, body(): pl.pallas_call(functools.partial(kernel, bands), out_shape=jax.ShapeDtype...  19.1 us
    unnamed x1, local copies, waits for them, and re-layouts  0.66 us

profile of v4, /device:TPU:0, one launch (start us, length us, event | category | flops | bytes accessed | tf_op | source)
XLA Modules:
  0.0 19.8 jit_solution(15324693634535078230)
XLA Ops:
  0.0 19.1 %layer.1 = bf16[255,256]{1,0:T(8,128)(2,1)S(1)} custom-call(bf16[255,256]{1,0:T(8,128)(2,1)} %feat_hbm.1, s32[255,512]{1,0:T(8,128)} %corners_hbm.1, f32[255,512]{1,0:T(8,128)} %bilinear_hbm.1, f32[255,128]{1,0:T(8,128)} %attention_hbm.1, bf16[256,256]{1,0:T(8,128)(2,1)} %w_value_hbm.1, f32[1,256]{1,0:T(1,128)} %bitcast.9, bf16[256,256]{1,0:T(8,128)(2,1)} %w_out_hbm.1, ...), custom_call_target="tpu_custom_call" | custom-call | tf_op jit(solution)/shard_map/layer/pallas_call | solution.py:477
  19.1 0.7 %copy.18 = bf16[255,256]{1,0:T(8,128)(2,1)} copy(bf16[255,256]{1,0:T(8,128)(2,1)S(1)} %layer.1) | data formatting | bytes 261120
